TPU v7x, 32 devices: a whole 2x2x4 slice. The times are simulated.
32 devices in a mesh: groups: 2 (over y), ctx: 4 (over z), ep: 2 (over x), tp: 2 (over core).
Axes of the slice: x: 2, y: 2, z: 4, core: 2. Of those that a mesh axis runs over, the one named last changes fastest.
Arguments:
- queries: bfloat16 [4, 512, 5120], P(('groups', 'ep'), 'ctx', 'tp'), parts along dimension 0, may hold values from -128 to 128
- keys: bfloat16 [4, 512, 1024], P(('groups', 'ep'), 'ctx', 'tp'), parts along dimension 0, may hold values from -6 to 6
- values: bfloat16 [4, 512, 1024], P(('groups', 'ep'), 'ctx', 'tp'), parts along dimension 0, may hold values from -6 to 6
- expert_ids: int32 [4, 512, 1], P(('groups', 'ep'), 'ctx'), parts along dimension 0, may hold values from 0 to 127, as said below
- router: bfloat16 [5120, 2], P('tp', 'ep'), may hold values from -0.3125 to 0.3125
- w_gate: bfloat16 [2, 5120, 4096], P('ep', 'tp', 'ctx'), may hold values from -0.3125 to 0.3125
- w_up: bfloat16 [2, 5120, 4096], P('ep', 'tp', 'ctx'), may hold values from -0.3125 to 0.3125
- w_down: bfloat16 [2, 4096, 5120], P('ep', 'ctx', 'tp'), may hold values from -0.09375 to 0.09375
Outputs:
- layer_out: bfloat16 [4, 512, 5120], P(('groups', 'ep'), 'ctx', 'tp'), parts along dimension 0
There are 2 independent parts, one for each index of `groups`. A program takes and returns all parts, laid end to end along the dimension named above; an argument that names none is the same for every part. Nothing has to cross between parts.
Inputs may be any that keep to these rules, and one draw needn't show every extreme that they name: `expert_ids`: among the positions of one device, each expert below 2 is named at most 2 times; in every draw one of them is named exactly 2 times on every device.
All inputs are finite; a program needn't handle non-finite values.
Results may differ from a plain program's by a relative error of at most 0.023.
Values may be sent and summed in bfloat16 or wider, within the bound.
A program may use at most 64 MiB of HBM per device.

v0:
```python
import jax
import jax.numpy as jnp
from jax import lax
from jax.sharding import PartitionSpec as P

HEAD_WIDTH = 128
CAP = 2


def block_width(key_count):
    for candidate in (512, 256, 128):
        return candidate
    return key_count


def fresh_state(query_rows, kv_heads, group_width):
    return (
        jnp.full((kv_heads, group_width, query_rows), -1e30, jnp.float32),
        jnp.zeros((kv_heads, group_width, query_rows), jnp.float32),
        jnp.zeros((query_rows, kv_heads, group_width, HEAD_WIDTH), jnp.float32),
    )


def absorb_block(status, query_half, query_pos, key_block, value_block, key_pos):
    old_max, totals, weighted = status
    scores = jnp.einsum(
        "rgqd,kgd->gqrk", query_half, key_block, preferred_element_type=jnp.float32
    ) * HEAD_WIDTH ** (-0.5)
    visible = query_pos[:, None] >= key_pos[None, :]
    scores = jnp.where(visible, scores, -1e30)
    running_max = jnp.maximum(old_max, jnp.max(scores, axis=3))
    factor = jnp.exp(old_max - running_max)
    weights = jnp.where(visible, jnp.exp(scores - running_max[..., None]), 0.0)
    totals = totals * factor + jnp.sum(weights, axis=3)
    update = jnp.einsum(
        "gqrk,kgd->rgqd",
        weights.astype(jnp.bfloat16),
        value_block,
        preferred_element_type=jnp.float32,
    )
    weighted = weighted * jnp.transpose(factor, (2, 0, 1))[..., None] + update
    return (running_max, totals, weighted)


def finish(status, row_count):
    old_max, totals, weighted = status
    normed = weighted / jnp.transpose(totals, (2, 0, 1))[..., None]
    return normed.astype(jnp.bfloat16).reshape(row_count, -1)


def shards(queries, keys, values, expert_ids, router, w_gate, w_up, w_down):
    row_count = queries.shape[1]
    half_rows = row_count // 2
    feature_width = queries.shape[2]
    kv_heads = keys.shape[2] // HEAD_WIDTH
    group_width = feature_width // HEAD_WIDTH // kv_heads
    ep_count = lax.axis_size("ep")
    ctx_place = lax.axis_index("ctx")
    local_queries = queries[0].reshape(row_count, kv_heads, group_width, HEAD_WIDTH)
    lead_half = local_queries[:half_rows]
    tail_half = local_queries[half_rows:]
    lead_pos = ctx_place * row_count + jnp.arange(half_rows, dtype=jnp.int32)
    tail_pos = ctx_place * row_count + half_rows + jnp.arange(half_rows, dtype=jnp.int32)
    initial = (
        fresh_state(half_rows, kv_heads, group_width),
        fresh_state(half_rows, kv_heads, group_width),
    )
    key_piece = lax.all_gather(keys, "ctx", axis=1, tiled=True)[0]
    key_count = key_piece.shape[0]
    key_block_rows = block_width(key_count)
    block_count = key_count // key_block_rows
    key_blocks = key_piece.reshape(block_count, key_block_rows, kv_heads, HEAD_WIDTH)
    value_blocks = lax.all_gather(values, "ctx", axis=1, tiled=True)[0].reshape(
        block_count, key_block_rows, kv_heads, HEAD_WIDTH
    )
    offsets = jnp.arange(block_count, dtype=jnp.int32) * key_block_rows

    def one_block(status, inputs):
        key_block, value_block, block_begin = inputs
        key_pos = block_begin + jnp.arange(key_block_rows, dtype=jnp.int32)
        lead_state = lax.cond(
            block_begin <= lead_pos[-1],
            lambda kept_state: absorb_block(
                kept_state, lead_half, lead_pos, key_block, value_block, key_pos
            ),
            lambda kept_state: kept_state,
            status[0],
        )
        tail_state = lax.cond(
            block_begin <= tail_pos[-1],
            lambda kept_state: absorb_block(
                kept_state, tail_half, tail_pos, key_block, value_block, key_pos
            ),
            lambda kept_state: kept_state,
            status[1],
        )
        return ((lead_state, tail_state), None)

    result, _ = lax.scan(one_block, initial, (key_blocks, value_blocks, offsets))
    lead_status, tail_status = result
    lead_out = finish(lead_status, half_rows)
    tail_out = finish(tail_status, half_rows)
    attended = jnp.concatenate([lead_out, tail_out], axis=0)
    chosen = expert_ids[0, :, 0]
    choose = (chosen[:, None] == jnp.arange(ep_count, dtype=jnp.int32)[None, :]).astype(jnp.int32)
    earlier = jnp.cumsum(choose, axis=0) - choose
    slot_index = jnp.sum(earlier * choose, axis=1)
    target = chosen * CAP + slot_index
    spread = (target[None, :] == jnp.arange(ep_count * CAP, dtype=jnp.int32)[:, None]).astype(
        jnp.bfloat16
    )
    outgoing = jnp.dot(spread, attended, preferred_element_type=jnp.float32).astype(jnp.bfloat16)
    arrived = lax.all_to_all(
        outgoing.reshape(ep_count, CAP, feature_width),
        "ep",
        split_axis=0,
        concat_axis=0,
        tiled=True,
    )
    gathered = lax.all_gather(arrived[None], "ctx", axis=0, tiled=True)
    members = gathered.reshape(-1, feature_width)
    gate_w = w_gate[0]
    up_w = w_up[0]
    down_w = w_down[0]
    gate_part = jnp.dot(members, gate_w, preferred_element_type=jnp.float32)
    up_part = jnp.dot(members, up_w, preferred_element_type=jnp.float32)
    score_part = jnp.dot(members, router, preferred_element_type=jnp.float32)
    gate_sum, up_sum, router_score = (
        lax.psum(gate_part.astype(jnp.bfloat16), "tp").astype(jnp.float32),
        lax.psum(up_part.astype(jnp.bfloat16), "tp").astype(jnp.float32),
        lax.psum(score_part.astype(jnp.bfloat16), "tp").astype(jnp.float32),
    )
    weight = jax.nn.sigmoid(router_score)
    hidden = (jax.nn.silu(weight * gate_sum) * (weight * up_sum)).astype(jnp.bfloat16)
    expert_rows = lax.psum_scatter(
        jnp.dot(hidden, down_w, preferred_element_type=jnp.float32).astype(jnp.bfloat16),
        "ctx",
        scatter_dimension=0,
        tiled=True,
    )
    returned = lax.all_to_all(
        expert_rows.reshape(ep_count, CAP, feature_width),
        "ep",
        split_axis=0,
        concat_axis=0,
        tiled=True,
    )
    returned = returned.reshape(ep_count * CAP, feature_width)
    routed = lax.dot_general(
        spread, returned, (((0,), (0,)), ((), ())), preferred_element_type=jnp.float32
    )
    layer_out = (attended.astype(jnp.float32) + routed).astype(jnp.bfloat16)
    return layer_out[None]


def solution(mesh):
    placed = (
        P(("groups", "ep"), "ctx", "tp"),
        P(("groups", "ep"), "ctx", "tp"),
        P(("groups", "ep"), "ctx", "tp"),
        P(("groups", "ep"), "ctx", None),
        P("tp", "ep"),
        P("ep", "tp", "ctx"),
        P("ep", "tp", "ctx"),
        P("ep", "ctx", "tp"),
    )
    return jax.shard_map(
        shards,
        mesh=mesh,
        in_specs=placed,
        out_specs=P(("groups", "ep"), "ctx", "tp"),
        check_vma=False,
    )
```

profile of v0, /device:TPU:0, one launch (start us, length us, event | category | flops | bytes accessed | tf_op | source)
XLA Modules:
  0.0 157.5 jit_solution(6667889364840034550)
XLA Ops:
  6.5 1.0 copy.23
  7.6 16.7 %all_gather.9 = bf16[1,512,512]{1,2,0:T(8,128)(2,1)S(1)} all-gather(bf16[1,128,512]{1,2,0:T(8,128)(2,1)S(1)} %copy.23), channel_id=1, replica_groups=mesh['groups'=2,'ctx'=4,'ep'=2,'tp'=2] {'ctx'}, dimensions={1}, use_global_device_ids=true | all-gather | bytes 655360 | tf_op jit(solution)/shard_map/all_gather | solution.py:68
  24.3 1.0 copy.24
  25.3 14.6 %all_gather.10 = bf16[1,512,512]{1,2,0:T(8,128)(2,1)S(1)} all-gather(bf16[1,128,512]{1,2,0:T(8,128)(2,1)S(1)} %copy.24), channel_id=1, replica_groups=mesh['groups'=2,'ctx'=4,'ep'=2,'tp'=2] {'ctx'}, dimensions={1}, use_global_device_ids=true | all-gather | bytes 655360 | tf_op jit(solution)/shard_map/all_gather | solution.py:73
  39.9 0.6 slice.23
  41.1 0.1 broadcast.44
  41.2 0.6 broadcast.43
  41.8 4.8 %conditional.3 = (f32[4,5,64]{2,1,0:T(8,128)S(1)}, f32[64,4,5,128]{3,0,2,1:T(8,128)S(1)}) conditional(s32[]{:T(128)} %bitcast.14, (f32[4,5,64]{2,1,0:T(8,128)}, f32[64,4,5,128]{3,0,2,1:T(8,128)S(1)}) %tuple.31, (s32[64]{0:T(128)S(1)}, s32[512]{0:T(512)S(1)}, bf16[1,128,2560]{2,1,0:T(8,128)(2,1)}, bf16[512,4,128]{0,2,1:T(8,128)(2,1)S(1)}, ...), branch_computations={%region_4.5_spmd, %region_5.0_spmd} | conditional | flops 344428288 | bytes 12067088 | solution.py:89
  41.8 0.1 broadcast_compare_fusion.1
  41.9 1.0 slice.18
  42.9 0.4 slice.19
  43.3 0.7 fusion.20
  44.0 0.9 fusion.22
  44.9 0.7 multiply_add_fusion.1
  45.6 1.1 fusion.29
  46.7 0.2 divide_convert_fusion
  46.9 0.2 copy.30
  47.2 0.4 reshape.57
  47.6 0.6 slice.22
  48.8 5.9 %conditional.2 = ((f32[4,5,64]{2,1,0:T(8,128)}, f32[64,4,5,128]{3,0,2,1:T(8,128)S(1)})) conditional(s32[]{:T(128)} %bitcast.10, (f32[4,5,64]{2,1,0:T(8,128)}, f32[64,4,5,128]{3,0,2,1:T(8,128)S(1)}) %tuple.31, (s32[64]{0:T(128)S(1)}, s32[512]{0:T(512)S(1)}, bf16[1,128,2560]{2,1,0:T(8,128)(2,1)S(1)}, bf16[512,4,128]{0,2,1:T(8,128)(2,1)S(1)}, ...), branch_computations={%region_0.1_spmd, %region_1.4_spmd} | conditional | flops 344428288 | bytes 12239212 | solution.py:81
  48.8 0.7 broadcast_compare_fusion
  49.6 0.4 slice.17
  50.0 1.4 fusion
  51.4 0.9 fusion.2
  52.3 1.3 multiply_add_fusion
  53.6 1.1 fusion.9
  54.7 1.0 divide_convert_fusion.1
  55.7 0.2 copy.27
  55.9 0.4 reshape.56
  56.4 0.1 fusion.59
  56.4 0.2 reduce_window_sum.11
  56.6 0.2 select_reduce_fusion
  56.8 0.2 convolution_convert_fusion
  57.1 6.4 %all_to_all.10 = bf16[2,2,2560]{2,1,0:T(2,128)(2,1)S(1)} all-to-all(bf16[2,2,2560]{2,1,0:T(2,128)(2,1)S(1)} %reshape.58), channel_id=1, replica_groups=mesh['groups'=2,'ctx'=4,'ep'=2,'tp'=2] {'ep'}, dimensions={0} | all-to-all | bytes 40960 | tf_op jit(solution)/shard_map/all_to_all | solution.py:113
  63.5 13.2 %all-gather = bf16[8,2,2560]{2,1,0:T(2,128)(2,1)S(1)} all-gather(bf16[2,2,2560]{2,1,0:T(2,128)(2,1)S(1)} %all_to_all.10), channel_id=2, replica_groups=mesh['groups'=2,'ctx'=4,'ep'=2,'tp'=2] {'ctx'}, dimensions={0}, use_global_device_ids=true | all-gather | bytes 102400 | tf_op jit(solution)/shard_map/all_gather | solution.py:120
  76.7 3.9 %fusion.51 = bf16[16,1024]{1,0:T(8,128)(2,1)} fusion(bf16[16,2560]{1,0:T(8,128)(2,1)S(1)} %reshape.59, bf16[1,2560,1024]{2,1,0:T(8,128)(2,1)} %param.17), kind=kOutput, calls=%fused_computation.51 | convolution fusion | flops 83902464 | bytes 5357568 | tf_op jit(solution)/shard_map/dot_general | solution.py:125
  80.6 3.9 %fusion.54 = bf16[16,1024]{1,0:T(8,128)(2,1)} fusion(bf16[16,2560]{1,0:T(8,128)(2,1)S(1)} %reshape.59, bf16[1,2560,1024]{2,1,0:T(8,128)(2,1)} %param.18), kind=kOutput, calls=%fused_computation.52 | convolution fusion | flops 83902464 | bytes 5357568 | tf_op jit(solution)/shard_map/dot_general | solution.py:126
  84.6 0.6 fusion.58
  85.2 0.0 all-reduce.7.cloned.1.call-update
  85.2 0.0 all-reduce.5.cloned.1.call-start
  85.3 16.5 %all-reduce.7.cloned.1.call-done = (bf16[16,1024]{1,0:T(8,128)(2,1)}, bf16[16,1024]{1,0:T(8,128)(2,1)}, bf16[16,1]{0,1:T(2,128)(2,1)}) async-done(((bf16[16,1024]{1,0:T(8,128)(2,1)}, bf16[16,1024]{1,0:T(8,128)(2,1)}, bf16[16,1]{0,1:T(2,128)(2,1)}), (bf16[16,1024]{1,0:T(8,128)(2,1)}, bf16[16,1024]{1,0:T(8,128)(2,1)}, bf16[16,1]{0,1:T(2,128)(2,1)})) %all-reduce.7.cloned.1.call-update) | async-done | bytes 65584 | tf_op jit(solution)/shard_map/psum | solution.py:130
  101.8 0.7 divide_bitcast_fusion
  102.5 4.0 %fusion.48 = bf16[16,2560]{1,0:T(8,128)(2,1)} fusion(bf16[1,1024,2560]{2,1,0:T(8,128)(2,1)} %param.19, bf16[16,1024]{1,0:T(8,128)(2,1)} %get-tuple-element.178, bf16[16,1024]{1,0:T(8,128)(2,1)} %get-tuple-element.179, f32[16]{0:T(128)S(1)} %divide_bitcast_fusion), kind=kOutput, calls=%fused_computation.49 | convolution fusion | flops 84090880 | bytes 5390400 | tf_op jit(solution)/shard_map/dot_general | solution.py:136
  106.6 0.6 dynamic-slice
  107.7 34.5 %all-reduce.5.cloned.1.call-done = bf16[16,2560]{1,0:T(8,128)(2,1)} async-done(((bf16[16,2560]{1,0:T(8,128)(2,1)}), bf16[16,2560]{1,0:T(8,128)(2,1)}) %all-reduce.5.cloned.1.call-update) | async-done | bytes 81936
  142.2 0.8 constant_dynamic-slice_fusion
  143.0 6.4 %all_to_all.11 = bf16[2,2,2560]{2,1,0:T(2,128)(2,1)S(1)} all-to-all(bf16[2,2,2560]{2,1,0:T(2,128)(2,1)S(1)} %reshape.61), channel_id=1, replica_groups=mesh['groups'=2,'ctx'=4,'ep'=2,'tp'=2] {'ep'}, dimensions={0} | all-to-all | bytes 40960 | tf_op jit(solution)/shard_map/all_to_all | solution.py:141
  149.5 1.2 fusion.47
  (31 shorter events, 0.3 us)
Async XLA Ops:
  6.5 78.0 %copy-start = (bf16[2560,1]{0,1:T(2,128)(2,1)S(1)}, bf16[2560,1]{0,1:T(2,128)(2,1)}, u32[]{:S(2)}) copy-start(bf16[2560,1]{0,1:T(2,128)(2,1)} %param.16) | copy-start | bytes 15364
  6.5 95.3 %all-reduce.7.cloned.1.call-start = ((), (), s32[]{:S(2)}) async-start(), calls=%async_computation.3 | async-start | bytes 132096 | tf_op jit(solution)/shard_map/psum | solution.py:130
  46.7 2.1 %copy-start.1 = (bf16[1,128,2560]{2,1,0:T(8,128)(2,1)S(1)}, bf16[1,128,2560]{2,1,0:T(8,128)(2,1)}, u32[]{:S(2)}) copy-start(bf16[1,128,2560]{2,1,0:T(8,128)(2,1)} %param.12) | copy-start | bytes 1966084
  48.8 0.7 copy-start.2
  49.6 1.8 %copy-start.3 = (f32[4,5,64]{2,1,0:T(8,128)S(1)}, f32[4,5,64]{2,1,0:T(8,128)}, u32[]{:S(2)}) copy-start(f32[4,5,64]{2,1,0:T(8,128)} %copy-done.2) | copy-start | bytes 15364 | tf_op jit(solution)/shard_map/while/body/eval_jaxpr/cond
  49.6 1.9 %copy-start.4 = (pred[64,512]{1,0:T(8,128)(4,1)S(1)}, pred[64,512]{1,0:T(8,128)(4,1)}, u32[]{:S(2)}) copy-start(pred[64,512]{1,0:T(8,128)(4,1)} %broadcast_compare_fusion) | copy-start | bytes 98308 | tf_op jit(solution)/shard_map/while/body/eval_jaxpr/cond
  54.7 1.6 %copy-start.5 = (s32[1,128,1]{1,2,0:T(1,128)S(1)}, s32[1,128,1]{1,2,0:T(1,128)}, u32[]{:S(2)}) copy-start(s32[1,128,1]{1,2,0:T(1,128)} %param.15) | copy-start | bytes 1540
  85.2 57.0 %all-reduce.5.cloned.1.call-start = ((), (), s32[]{:S(2)}) async-start(), calls=%async_computation.2 | async-start | bytes 163840
  102.5 4.1 %copy-start.6 = (u32[32]{0:T(128)S(1)}, u32[32]{0:T(128)}, u32[]{:S(2)}) copy-start(u32[32]{0:T(128)} %constant.73) | copy-start | bytes 388
Sparse Core Ops, SparseCore 0:
  85.3 16.4 all-reduce.6
  106.7 35.4 all-reduce.4
where the time goes:
time: 158 us
  blocking collectives  57.4 us (36%)
  waiting for transfers between devices  51.1 us (32%)
  matrix products  18.1 us (11%)
  between operations  15.5 us (10%)
  local copies, waits for them, and re-layouts  8.44 us (5%)
  other arithmetic  6.94 us (4%)
    unnamed x3, waiting for transfers between devices  34.5 us
    all_gather x1, blocking collectives, shards(): key_piece = lax.all_gather(keys, 'ctx', axis=1, tiled=True)[0]  16.7 us
    psum x1, waiting for transfers between devices, shards(): lax.psum(up_part.astype(jnp.bfloat16), 'tp').astype(jnp.float32)  16.5 us
    all_gather x1, blocking collectives, shards(): lax.all_gather(values, 'ctx', axis=1, tiled=True)[0]  14.6 us
    all_gather x1, blocking collectives, shards(): gathered = lax.all_gather(arrived[None], 'ctx', axis=0, tiled=True)  13.2 us
    all_to_all x1, blocking collectives, shards(): lax.all_to_all(outgoing.reshape(ep_count, CAP, feature_width), 'ep', spli...  6.44 us
    all_to_all x1, blocking collectives, shards(): lax.all_to_all(expert_rows.reshape(ep_count, CAP, feature_width), 'ep', s...  6.41 us
    dot_general x1, matrix products, shards(): jnp.dot(hidden, down_w, preferred_element_type=jnp.float32)  4.03 us
  transfers between devices with their start and end apart: 2, of which 2 were waited for; matrix products, arithmetic and copies ran while one was open for 0% of the time, Pallas kernels for 0%

commit v1 on v0

v1 whole, which is shorter than its diff:
```python
import functools
import math

import jax
import jax.numpy as jnp
from jax import lax
from jax.experimental import pallas as pl
from jax.experimental.pallas import tpu as pltpu
from jax.sharding import PartitionSpec as P

HEAD_WIDTH = 128
CAP = 2
MESH = pl.DeviceIdType.MESH
MASKED = -1e30
EXP2_SCALE = HEAD_WIDTH ** (-0.5) * math.log2(math.e)


def tiles_of(width, tile):
    tile = min(width, tile)
    return [(start, min(tile, width - start)) for start in range(0, width, tile)]


def each(count, body):
    if count <= 8:
        for index in range(count):
            body(index)
    else:
        pl.loop(0, count)(body)


def kernel(
    n_ctx, n_ep, n_tp,
    ids_ref, router_ref, q_ref, k_ref, v_ref, wg_hbm, wu_hbm, wd_hbm,
    out_ref,
    wg, wu, wd, kbuf, vbuf, acc, row_max, totals, att,
    out_rows, in_rows, members_f32, part, part_in, score, score_in, hidden,
    down_out, down_in, returned,
    w_sem, kv_send, kv_recv, row_send, row_recv, part_send, part_recv, score_sem,
    down_send, down_recv,
):
    ctx = lax.axis_index("ctx")
    ep = lax.axis_index("ep")
    tp = lax.axis_index("tp")
    n = n_ctx * n_ep
    me = ep * n_ctx + ctx
    rows = q_ref.shape[1]
    features = q_ref.shape[2]
    kv_heads = k_ref.shape[2] // HEAD_WIDTH
    group = features // HEAD_WIDTH // kv_heads
    half = rows // 2
    fan = n_ctx // 2
    hidden_width = wg.shape[1]
    chunk_count, _, double_width = part.shape
    chunk_width = double_width // 2
    slots = returned.shape[0]

    w_copies = [
        pltpu.make_async_copy(src.at[0], dst, w_sem.at[index])
        for index, (src, dst) in enumerate(((wg_hbm, wg), (wu_hbm, wu), (wd_hbm, wd)))
    ]
    for copy in w_copies:
        copy.start()

    barrier = pltpu.get_barrier_semaphore()

    def greet(other):
        @pl.when(other != me)
        def _():
            pl.semaphore_signal(
                barrier, inc=1,
                device_id={"ep": other // n_ctx, "ctx": other % n_ctx},
                device_id_type=MESH,
            )

    each(n, greet)
    for step in range(1, n_tp):
        pl.semaphore_signal(
            barrier, inc=1, device_id={"tp": (tp + step) % n_tp}, device_id_type=MESH
        )
    pl.semaphore_wait(barrier, n - 1 + n_tp - 1)

    right = (ctx + 1) % n_ctx
    left = (ctx + n_ctx - 1) % n_ctx

    def kv_copies(block, piece, direction, own):
        span = pl.ds(piece * half, half)
        target = right if direction == 0 else left
        result = []
        for index, (src, buf) in enumerate(((k_ref, kbuf), (v_ref, vbuf))):
            origin = src.at[0, span] if own else buf.at[block, span]
            result.append(
                pltpu.make_async_remote_copy(
                    src_ref=origin,
                    dst_ref=buf.at[block, span],
                    send_sem=kv_send.at[direction, block, piece, index],
                    recv_sem=kv_recv.at[block, piece, index],
                    device_id={"ctx": target},
                    device_id_type=MESH,
                )
            )
        return result

    def send_kv(block, piece, direction, own=False):
        for copy in kv_copies(block, piece, direction, own):
            copy.start()

    def wait_kv(block, piece):
        for copy in kv_copies(block, piece, 0, False):
            copy.wait_recv()

    send_kv(ctx, 0, 0, True)
    send_kv(ctx, 1, 1, True)
    if fan > 1:
        send_kv(ctx, 1, 0, True)
        send_kv(ctx, 0, 1, True)

    kbuf[ctx] = k_ref[0]
    vbuf[ctx] = v_ref[0]
    acc[...] = jnp.zeros_like(acc)
    totals[...] = jnp.zeros_like(totals)
    row_max[...] = jnp.full_like(row_max, MASKED)

    ids = ids_ref[...]
    slot_row = lax.broadcasted_iota(jnp.int32, (slots, rows), 0)
    choose = jnp.where(ids == slot_row, 1.0, 0.0)
    below = lax.broadcasted_iota(jnp.int32, (rows, rows), 0)
    across = lax.broadcasted_iota(jnp.int32, (rows, rows), 1)
    strict = jnp.where(below < across, 1.0, 0.0).astype(jnp.bfloat16)
    earlier = jnp.dot(choose.astype(jnp.bfloat16), strict, preferred_element_type=jnp.float32)
    slot_index = jnp.sum(earlier * choose, axis=0, keepdims=True).astype(jnp.int32)
    target_row = jnp.where(ids < n_ep, ids * CAP + slot_index, -1)
    spread = jnp.where(target_row == slot_row, 1.0, 0.0).astype(jnp.bfloat16)
    query_offset = lax.broadcasted_iota(jnp.int32, (rows, rows), 0)
    key_offset = lax.broadcasted_iota(jnp.int32, (rows, rows), 1)
    offset_gap = query_offset - key_offset

    def process(block):
        visible = offset_gap >= (block - ctx) * rows
        visible = jnp.concatenate([visible] * group, axis=0)
        for head in range(kv_heads):
            lanes = slice(head * HEAD_WIDTH, (head + 1) * HEAD_WIDTH)
            stacked = jnp.concatenate(
                [
                    q_ref[0, :, (head * group + j) * HEAD_WIDTH:(head * group + j + 1) * HEAD_WIDTH]
                    for j in range(group)
                ],
                axis=0,
            )
            raw = lax.dot_general(
                stacked, kbuf[block, :, lanes], (((1,), (1,)), ((), ())),
                preferred_element_type=jnp.float32,
            )
            raw = jnp.where(visible, raw, MASKED)
            old_max = row_max[head]
            new_max = jnp.maximum(old_max, jnp.max(raw, axis=1, keepdims=True))
            factor = jnp.exp2((old_max - new_max) * EXP2_SCALE)
            weights = jnp.exp2((raw - new_max[:, :rows]) * EXP2_SCALE)
            row_max[head] = new_max
            totals[head] = totals[head] * factor + jnp.sum(weights, axis=1, keepdims=True)
            update = jnp.dot(
                weights.astype(jnp.bfloat16), vbuf[block, :, lanes],
                preferred_element_type=jnp.float32,
            )
            acc[head] = acc[head] * factor + update

    def visit(index, carry):
        step = (index + 1) // 2

        @pl.when((index % 2 == 1) & (index < n_ctx - 1))
        def _():
            from_left = (ctx + n_ctx - step) % n_ctx
            from_right = (ctx + step) % n_ctx
            wait_kv(from_left, 0)
            send_kv(from_left, 0, 0)
            wait_kv(from_right, 1)
            send_kv(from_right, 1, 1)
            wait_kv(from_left, 1)

            @pl.when(step + 1 < fan)
            def _():
                send_kv(from_left, 1, 0)

            wait_kv(from_right, 0)

            @pl.when(step + 1 < fan)
            def _():
                send_kv(from_right, 0, 1)

        block = jnp.where(index % 2 == 1, ctx + n_ctx - step, ctx + step) % n_ctx

        @pl.when(index == n_ctx - 1)
        def _():
            wait_kv(block, 0)
            wait_kv(block, 1)

        @pl.when(block <= ctx)
        def _():
            process(block)

        return carry

    lax.fori_loop(0, n_ctx, visit, 0)

    for head in range(kv_heads):
        normed = (acc[head] / totals[head]).astype(jnp.bfloat16)
        for j in range(group):
            place = (head * group + j) * HEAD_WIDTH
            att[:, place:place + HEAD_WIDTH] = normed[j * rows:(j + 1) * rows]

    for start, size in tiles_of(features, 512):
        picked = jnp.dot(
            spread, att[:, start:start + size], preferred_element_type=jnp.float32
        )
        for expert in range(n_ep):
            out_rows[expert, :, start:start + size] = picked[
                expert * CAP:(expert + 1) * CAP
            ].astype(jnp.bfloat16)

    def row_copy(other, source):
        return pltpu.make_async_remote_copy(
            src_ref=out_rows.at[other // n_ctx],
            dst_ref=in_rows.at[source],
            send_sem=row_send.at[other],
            recv_sem=row_recv.at[source],
            device_id={"ep": other // n_ctx, "ctx": other % n_ctx},
            device_id_type=MESH,
        )

    def others(body):
        def one(step):
            @pl.when(step != me)
            def _():
                body(step)

        each(n, one)

    others(lambda other: row_copy(other, me).start())
    in_rows[me] = out_rows[ep]
    for copy in w_copies:
        copy.wait()
    others(lambda other: row_copy(other, other).wait_recv())

    def gather_member(index):
        members_f32[index * CAP:(index + 1) * CAP, :] = in_rows[index].astype(jnp.float32)

    for index in range(n):
        gather_member(index)
    wide = members_f32[...]
    members = wide.astype(jnp.bfloat16)
    own_score = jnp.sum(wide * router_ref[...].astype(jnp.float32), axis=1, keepdims=True)
    score[...] = jnp.broadcast_to(own_score, score.shape).astype(jnp.bfloat16)
    peer = {"tp": n_tp - 1 - tp}
    score_copy = pltpu.make_async_remote_copy(
        src_ref=score, dst_ref=score_in, send_sem=score_sem.at[0], recv_sem=score_sem.at[1],
        device_id=peer, device_id_type=MESH,
    )
    score_copy.start()
    part_copies = []
    for chunk in range(chunk_count):
        span = slice(chunk * chunk_width, (chunk + 1) * chunk_width)
        part[chunk, :, :chunk_width] = jnp.dot(
            members, wg[:, span], preferred_element_type=jnp.float32
        ).astype(jnp.bfloat16)
        part[chunk, :, chunk_width:] = jnp.dot(
            members, wu[:, span], preferred_element_type=jnp.float32
        ).astype(jnp.bfloat16)
        copy = pltpu.make_async_remote_copy(
            src_ref=part.at[chunk], dst_ref=part_in.at[chunk],
            send_sem=part_send.at[chunk], recv_sem=part_recv.at[chunk],
            device_id=peer, device_id_type=MESH,
        )
        copy.start()
        part_copies.append(copy)
    score_copy.wait()
    gain = jax.nn.sigmoid(
        score[:, :1].astype(jnp.float32) + score_in[:, :1].astype(jnp.float32)
    )
    for chunk, copy in enumerate(part_copies):
        copy.wait()
        both = part[chunk].astype(jnp.float32) + part_in[chunk].astype(jnp.float32)
        gate = gain * both[:, :chunk_width]
        up = gain * both[:, chunk_width:]
        hidden[:, chunk * chunk_width:(chunk + 1) * chunk_width] = (
            gate * jax.nn.sigmoid(gate) * up
        ).astype(jnp.bfloat16)
    for start, size in tiles_of(features, 512):
        product = jnp.dot(
            hidden[...], wd[:, start:start + size], preferred_element_type=jnp.float32
        )
        for index in range(n):
            down_out[index, :, start:start + size] = product[
                index * CAP:(index + 1) * CAP
            ].astype(jnp.bfloat16)

    def down_copy(other, source):
        return pltpu.make_async_remote_copy(
            src_ref=down_out.at[other],
            dst_ref=down_in.at[source],
            send_sem=down_send.at[other],
            recv_sem=down_recv.at[source],
            device_id={"ep": other // n_ctx, "ctx": other % n_ctx},
            device_id_type=MESH,
        )

    others(lambda other: down_copy(other, me).start())
    down_in[me] = down_out[me]
    returned[...] = jnp.zeros_like(returned)

    others(lambda other: row_copy(other, me).wait_send())
    for copy in kv_copies(ctx, 0, 0, True) + kv_copies(ctx, 1, 1, True):
        copy.wait_send()
    if fan > 1:
        for copy in kv_copies(ctx, 1, 0, True) + kv_copies(ctx, 0, 1, True):
            copy.wait_send()

    def drain(step, carry):
        from_left = (ctx + n_ctx - step) % n_ctx
        from_right = (ctx + step) % n_ctx
        for copy in kv_copies(from_left, 0, 0, False) + kv_copies(from_right, 1, 1, False):
            copy.wait_send()

        @pl.when(step + 1 < fan)
        def _():
            for copy in kv_copies(from_left, 1, 0, False) + kv_copies(from_right, 0, 1, False):
                copy.wait_send()

        return carry

    lax.fori_loop(1, fan, drain, 0)

    others(lambda other: down_copy(other, other).wait_recv())
    for expert in range(n_ep):
        total = down_in[expert * n_ctx].astype(jnp.float32)
        for index in range(1, n_ctx):
            total = total + down_in[expert * n_ctx + index].astype(jnp.float32)
        returned[expert * CAP:(expert + 1) * CAP, :] = total.astype(jnp.bfloat16).astype(jnp.float32)
    for start, size in tiles_of(features, 512):
        routed = lax.dot_general(
            spread, returned[:, start:start + size].astype(jnp.bfloat16),
            (((0,), (0,)), ((), ())), preferred_element_type=jnp.float32,
        )
        out_ref[0, :, start:start + size] = (
            att[:, start:start + size].astype(jnp.float32) + routed
        ).astype(jnp.bfloat16)
    others(lambda other: down_copy(other, me).wait_send())


def shards(queries, keys, values, expert_ids, router, w_gate, w_up, w_down):
    n_ctx, n_ep, n_tp = (lax.axis_size(axis) for axis in ("ctx", "ep", "tp"))
    n = n_ctx * n_ep
    _, rows, features = queries.shape
    kv_width = keys.shape[2]
    kv_heads = kv_width // HEAD_WIDTH
    group = features // kv_width
    hidden_width = w_gate.shape[2]
    chunk_width = min(hidden_width, 256)
    chunk_count = hidden_width // chunk_width
    members = n * CAP
    slots = -(-n_ep * CAP // 8) * 8
    bf16, f32 = jnp.bfloat16, jnp.float32
    vmem = pl.BlockSpec(memory_space=pltpu.VMEM)
    hbm = pl.BlockSpec(memory_space=pl.ANY)
    dma = pltpu.SemaphoreType.DMA
    return pl.pallas_call(
        functools.partial(kernel, n_ctx, n_ep, n_tp),
        out_shape=jax.ShapeDtypeStruct(queries.shape, bf16),
        in_specs=[vmem] * 5 + [hbm] * 3,
        out_specs=vmem,
        scratch_shapes=[
            pltpu.VMEM(w_gate.shape[1:], bf16),
            pltpu.VMEM(w_up.shape[1:], bf16),
            pltpu.VMEM(w_down.shape[1:], bf16),
            pltpu.VMEM((n_ctx, rows, kv_width), bf16),
            pltpu.VMEM((n_ctx, rows, kv_width), bf16),
            pltpu.VMEM((kv_heads, group * rows, HEAD_WIDTH), f32),
            pltpu.VMEM((kv_heads, group * rows, HEAD_WIDTH), f32),
            pltpu.VMEM((kv_heads, group * rows, HEAD_WIDTH), f32),
            pltpu.VMEM((rows, features), bf16),
            pltpu.VMEM((n_ep, CAP, features), bf16),
            pltpu.VMEM((n, CAP, features), bf16),
            pltpu.VMEM((members, features), f32),
            pltpu.VMEM((chunk_count, members, 2 * chunk_width), bf16),
            pltpu.VMEM((chunk_count, members, 2 * chunk_width), bf16),
            pltpu.VMEM((members, 128), bf16),
            pltpu.VMEM((members, 128), bf16),
            pltpu.VMEM((members, hidden_width), bf16),
            pltpu.VMEM((n, CAP, features), bf16),
            pltpu.VMEM((n, CAP, features), bf16),
            pltpu.VMEM((slots, features), f32),
            dma((3,)),
            dma((2, n_ctx, 2, 2)),
            dma((n_ctx, 2, 2)),
            dma((n,)),
            dma((n,)),
            dma((chunk_count,)),
            dma((chunk_count,)),
            dma((2,)),
            dma((n,)),
            dma((n,)),
        ],
        compiler_params=pltpu.CompilerParams(
            collective_id=0, has_side_effects=True, vmem_limit_bytes=60 * 1024 * 1024
        ),
    )(
        expert_ids.reshape(1, rows), router.reshape(1, features), queries, keys, values,
        w_gate, w_up, w_down,
    )


def solution(mesh):
    placed = (
        P(("groups", "ep"), "ctx", "tp"),
        P(("groups", "ep"), "ctx", "tp"),
        P(("groups", "ep"), "ctx", "tp"),
        P(("groups", "ep"), "ctx", None),
        P("tp", "ep"),
        P("ep", "tp", "ctx"),
        P("ep", "tp", "ctx"),
        P("ep", "ctx", "tp"),
    )
    return jax.shard_map(
        shards,
        mesh=mesh,
        in_specs=placed,
        out_specs=P(("groups", "ep"), "ctx", "tp"),
        check_vma=False,
    )
```

time: 158 us -> 43.2 us (0.27)
  blocking collectives: 57.4 us -> 0 us
  waiting for transfers between devices: 51.1 us -> 0 us
  Pallas kernels: 0 us -> 41.1 us
  matrix products: 18.1 us -> 0 us
  between operations: 15.5 us -> 0.01 us
  other arithmetic: 6.94 us -> 0 us
  local copies, waits for them, and re-layouts: 8.44 us -> 1.97 us
    all_gather x3 -> x0, blocking collectives: 44.5 us -> none  [the longest x1 16.7 us: shards(): key_piece = lax.all_gather(keys, 'ctx', axis=1, tiled=True)[0]]
    pallas_call x0 -> x1, Pallas kernels: none -> 41.1 us  [shards(): pl.pallas_call(functools.partial(kernel, n_ctx, n_ep, n_tp), out_shape=ja...]
    unnamed x3 -> x0, waiting for transfers between devices: 34.5 us -> none
    dot_general x10 -> x0, matrix products: 18.1 us -> none  [the longest x1 4.03 us: shards(): jnp.dot(hidden, down_w, preferred_element_type=jnp.float32)]
    psum x1 -> x0, waiting for transfers between devices: 16.5 us -> none  [shards(): lax.psum(up_part.astype(jnp.bfloat16), 'tp').astype(jnp.float32)]
    all_to_all x2 -> x0, blocking collectives: 12.9 us -> none  [the longest x1 6.44 us: shards(): lax.all_to_all(outgoing.reshape(ep_count, CAP, feature_width), 'ep', spli...]
    slice x6 -> x0, local copies, waits for them, and re-layouts: 2.97 us -> none  [the longest x2 1.39 us: shards(): tail_half = local_queries[half_rows:]]
    add x5 -> x0, other arithmetic: 2.07 us -> none  [the longest x2 2.06 us: absorb_block(): totals = totals * factor + jnp.sum(weights, axis=3)]
  transfers between devices with their start and end apart: 2 -> 0, of which waited for: 2 -> 0; matrix products, arithmetic and copies ran while one was open for 0% -> 0% of each run, Pallas kernels for 0% -> 0%
where the time goes in v1:
time: 43.2 us; the launch traced here: 43 us
  Pallas kernels  41.1 us (95%)
  local copies, waits for them, and re-layouts  1.97 us (5%)
    pallas_call x1, Pallas kernels, shards(): pl.pallas_call(functools.partial(kernel, n_ctx, n_ep, n_tp), out_shape=ja...  41.1 us
    unnamed x1, local copies, waits for them, and re-layouts  1.97 us

profile of v1, /device:TPU:0, one launch (start us, length us, event | category | flops | bytes accessed | tf_op | source)
XLA Modules:
  0.0 43.0 jit_solution(16369636162471890293)
XLA Ops:
  0.0 41.1 %shard_map.82 = bf16[1,128,2560]{2,1,0:T(8,128)(2,1)} custom-call(s32[1,128]{1,0:T(1,128)} %bitcast.3, bf16[1,2560]{1,0:T(2,128)(2,1)} %bitcast.2, bf16[1,128,2560]{2,1,0:T(8,128)(2,1)} %q_ref.1, bf16[1,128,512]{2,1,0:T(8,128)(2,1)} %k_ref.1, bf16[1,128,512]{2,1,0:T(8,128)(2,1)} %v_ref.1, bf16[1,2560,1024]{2,1,0:T(8,128)(2,1)} %wg_hbm.1, ...), custom_call_target="tpu_custom_call" | custom-call | tf_op jit(solution)/shard_map/pallas_call | solution.py:364
  41.1 2.0 %copy.10 = bf16[1,128,2560]{2,1,0:T(8,128)(2,1)} copy(bf16[1,128,2560]{2,1,0:T(8,128)(2,1)} %shard_map.82) | data formatting | bytes 1310720

commit v2 on v1

--- a/solution.py
+++ b/solution.py
@@ -33,10 +33,10 @@
     ids_ref, router_ref, q_ref, k_ref, v_ref, wg_hbm, wu_hbm, wd_hbm,
     out_ref,
     wg, wu, wd, kbuf, vbuf, acc, row_max, totals, att,
-    out_rows, in_rows, members_f32, part, part_in, score, score_in, hidden,
+    q_out, q_in, q_all, part_out, part_got, part_all, lse_out, lse_in, lse_all, out_rows, in_rows, members_f32, part, part_in, score, score_in, hidden,
     down_out, down_in, returned,
     w_sem, kv_send, kv_recv, row_send, row_recv, part_send, part_recv, score_sem,
-    down_send, down_recv,
+    down_send, down_recv, q_send, q_recv, back_send, back_recv, lse_send, lse_recv,
 ):
     ctx = lax.axis_index("ctx")
     ep = lax.axis_index("ep")
@@ -61,65 +61,6 @@
     for copy in w_copies:
         copy.start()
 
-    barrier = pltpu.get_barrier_semaphore()
-
-    def greet(other):
-        @pl.when(other != me)
-        def _():
-            pl.semaphore_signal(
-                barrier, inc=1,
-                device_id={"ep": other // n_ctx, "ctx": other % n_ctx},
-                device_id_type=MESH,
-            )
-
-    each(n, greet)
-    for step in range(1, n_tp):
-        pl.semaphore_signal(
-            barrier, inc=1, device_id={"tp": (tp + step) % n_tp}, device_id_type=MESH
-        )
-    pl.semaphore_wait(barrier, n - 1 + n_tp - 1)
-
-    right = (ctx + 1) % n_ctx
-    left = (ctx + n_ctx - 1) % n_ctx
-
-    def kv_copies(block, piece, direction, own):
-        span = pl.ds(piece * half, half)
-        target = right if direction == 0 else left
-        result = []
-        for index, (src, buf) in enumerate(((k_ref, kbuf), (v_ref, vbuf))):
-            origin = src.at[0, span] if own else buf.at[block, span]
-            result.append(
-                pltpu.make_async_remote_copy(
-                    src_ref=origin,
-                    dst_ref=buf.at[block, span],
-                    send_sem=kv_send.at[direction, block, piece, index],
-                    recv_sem=kv_recv.at[block, piece, index],
-                    device_id={"ctx": target},
-                    device_id_type=MESH,
-                )
-            )
-        return result
-
-    def send_kv(block, piece, direction, own=False):
-        for copy in kv_copies(block, piece, direction, own):
-            copy.start()
-
-    def wait_kv(block, piece):
-        for copy in kv_copies(block, piece, 0, False):
-            copy.wait_recv()
-
-    send_kv(ctx, 0, 0, True)
-    send_kv(ctx, 1, 1, True)
-    if fan > 1:
-        send_kv(ctx, 1, 0, True)
-        send_kv(ctx, 0, 1, True)
-
-    kbuf[ctx] = k_ref[0]
-    vbuf[ctx] = v_ref[0]
-    acc[...] = jnp.zeros_like(acc)
-    totals[...] = jnp.zeros_like(totals)
-    row_max[...] = jnp.full_like(row_max, MASKED)
-
     ids = ids_ref[...]
     slot_row = lax.broadcasted_iota(jnp.int32, (slots, rows), 0)
     choose = jnp.where(ids == slot_row, 1.0, 0.0)
@@ -130,6 +71,124 @@
     slot_index = jnp.sum(earlier * choose, axis=0, keepdims=True).astype(jnp.int32)
     target_row = jnp.where(ids < n_ep, ids * CAP + slot_index, -1)
     spread = jnp.where(target_row == slot_row, 1.0, 0.0).astype(jnp.bfloat16)
+    live = n_ep * CAP
+    lane_row = lax.broadcasted_iota(jnp.int32, (slots, rows), 1)
+    row_place = jnp.sum(
+        jnp.where(target_row == slot_row, lane_row, 0), axis=1, keepdims=True
+    )
+    q_all[...] = jnp.zeros_like(q_all)
+    own_span = pl.ds(pl.multiple_of(ctx * slots, 8), slots)
+    for start, size in tiles_of(features, 512):
+        picked = jnp.dot(
+            spread, q_ref[0, :, start:start + size], preferred_element_type=jnp.float32
+        )
+        q_all[own_span, start:start + size] = picked
+        q_out[:, start:start + size] = picked[:live].astype(jnp.bfloat16)
+
+    barrier = pltpu.get_barrier_semaphore()
+
+    def greet(other):
+        @pl.when(other != me)
+        def _():
+            pl.semaphore_signal(
+                barrier, inc=1,
+                device_id={"ep": other // n_ctx, "ctx": other % n_ctx},
+                device_id_type=MESH,
+            )
+
+    each(n, greet)
+    for step in range(1, n_tp):
+        pl.semaphore_signal(
+            barrier, inc=1, device_id={"tp": (tp + step) % n_tp}, device_id_type=MESH
+        )
+    pl.semaphore_wait(barrier, n - 1 + n_tp - 1)
+
+    def own_copy(piece):
+        origin, buf = (k_ref, kbuf) if piece < 2 else (v_ref, vbuf)
+        span = pl.ds((piece % 2) * half, half)
+        return pltpu.make_async_remote_copy(
+            src_ref=origin.at[0, span],
+            dst_ref=buf.at[ctx, span],
+            send_sem=kv_send.at[ctx, piece],
+            recv_sem=kv_recv.at[ctx, piece],
+            device_id={"ctx": ctx + 1},
+            device_id_type=MESH,
+        )
+
+    def block_piece(block, piece):
+        buf = kbuf if piece < 2 else vbuf
+        span = pl.ds((piece % 2) * half, half)
+        return pltpu.make_async_remote_copy(
+            src_ref=buf.at[block, span],
+            dst_ref=buf.at[block, span],
+            send_sem=kv_send.at[block, piece],
+            recv_sem=kv_recv.at[block, piece],
+            device_id={"ctx": ctx + 1},
+            device_id_type=MESH,
+        )
+
+    def push_own(first, last):
+        @pl.when(ctx < n_ctx - 1)
+        def _():
+            for piece in range(first, last):
+                own_copy(piece).start()
+
+    def relay(block, first, last):
+        @pl.when(block >= 0)
+        def _():
+            for piece in range(first, last):
+                copy = block_piece(block, piece)
+                copy.wait_recv()
+
+                @pl.when(ctx < n_ctx - 1)
+                def _():
+                    copy.start()
+
+    def q_copy(source, target):
+        return pltpu.make_async_remote_copy(
+            src_ref=q_out, dst_ref=q_in.at[source],
+            send_sem=q_send.at[target], recv_sem=q_recv.at[source],
+            device_id={"ctx": target}, device_id_type=MESH,
+        )
+
+    def back_copies(source, target):
+        return [
+            pltpu.make_async_remote_copy(
+                src_ref=out.at[target], dst_ref=into.at[source],
+                send_sem=sent.at[target], recv_sem=got.at[source],
+                device_id={"ctx": target}, device_id_type=MESH,
+            )
+            for out, into, sent, got in (
+                (part_out, part_got, back_send, back_recv),
+                (lse_out, lse_in, lse_send, lse_recv),
+            )
+        ]
+
+    def lower(body):
+        def one(other):
+            @pl.when(other < ctx)
+            def _():
+                body(other)
+
+        each(n_ctx, one)
+
+    def upper(body):
+        def one(other):
+            @pl.when(other > ctx)
+            def _():
+                body(other)
+
+        each(n_ctx, one)
+
+    lower(lambda other: q_copy(ctx, other).start())
+    push_own(0, 2)
+
+    kbuf[ctx] = k_ref[0]
+    vbuf[ctx] = v_ref[0]
+    acc[...] = jnp.zeros_like(acc)
+    totals[...] = jnp.zeros_like(totals)
+    row_max[...] = jnp.full_like(row_max, MASKED)
+
     query_offset = lax.broadcasted_iota(jnp.int32, (rows, rows), 0)
     key_offset = lax.broadcasted_iota(jnp.int32, (rows, rows), 1)
     offset_gap = query_offset - key_offset
@@ -163,58 +222,94 @@
             )
             acc[head] = acc[head] * factor + update
 
-    def visit(index, carry):
-        step = (index + 1) // 2
-
-        @pl.when((index % 2 == 1) & (index < n_ctx - 1))
-        def _():
-            from_left = (ctx + n_ctx - step) % n_ctx
-            from_right = (ctx + step) % n_ctx
-            wait_kv(from_left, 0)
-            send_kv(from_left, 0, 0)
-            wait_kv(from_right, 1)
-            send_kv(from_right, 1, 1)
-            wait_kv(from_left, 1)
-
-            @pl.when(step + 1 < fan)
-            def _():
-                send_kv(from_left, 1, 0)
-
-            wait_kv(from_right, 0)
-
-            @pl.when(step + 1 < fan)
-            def _():
-                send_kv(from_right, 0, 1)
-
-        block = jnp.where(index % 2 == 1, ctx + n_ctx - step, ctx + step) % n_ctx
-
-        @pl.when(index == n_ctx - 1)
-        def _():
-            wait_kv(block, 0)
-            wait_kv(block, 1)
-
-        @pl.when(block <= ctx)
-        def _():
-            process(block)
-
-        return carry
-
-    lax.fori_loop(0, n_ctx, visit, 0)
-
+    part_all[...] = jnp.zeros_like(part_all)
+    lse_all[...] = jnp.full_like(lse_all, MASKED)
+    source_row = lax.broadcasted_iota(jnp.int32, (n_ctx * slots, 1), 0) // slots
+    limit = jnp.where(
+        source_row == ctx, jnp.concatenate([row_place] * n_ctx, axis=0), rows
+    )
+    limit = jnp.concatenate([limit] * group, axis=0)
+    upper(lambda other: q_copy(other, other).wait_recv())
+
+    for other in range(n_ctx):
+        @pl.when(other > ctx)
+        def _():
+            q_all[other * slots:other * slots + live, :] = q_in[other].astype(jnp.float32)
+
+    tall = n_ctx * slots
+    key_lane = lax.broadcasted_iota(jnp.int32, (group * tall, rows), 1)
+    seen = key_lane <= limit
+    head_lane = lax.broadcasted_iota(jnp.int32, (tall, 128), 1)
+    lse = jnp.zeros((tall, 128), jnp.float32)
     for head in range(kv_heads):
-        normed = (acc[head] / totals[head]).astype(jnp.bfloat16)
+        lanes = slice(head * HEAD_WIDTH, (head + 1) * HEAD_WIDTH)
+        stacked = jnp.concatenate(
+            [
+                q_all[:, (head * group + j) * HEAD_WIDTH:(head * group + j + 1) * HEAD_WIDTH]
+                for j in range(group)
+            ],
+            axis=0,
+        ).astype(jnp.bfloat16)
+        raw = lax.dot_general(
+            stacked, k_ref[0, :, lanes], (((1,), (1,)), ((), ())),
+            preferred_element_type=jnp.float32,
+        )
+        raw = jnp.where(seen, raw, MASKED)
+        top = jnp.max(raw, axis=1, keepdims=True)
+        weights = jnp.exp2((raw - top) * EXP2_SCALE)
+        total = jnp.sum(weights, axis=1, keepdims=True)
+        mixed = jnp.dot(
+            weights.astype(jnp.bfloat16), v_ref[0, :, lanes],
+            preferred_element_type=jnp.float32,
+        ) / total
+        column = top * EXP2_SCALE + jnp.log2(total)
         for j in range(group):
-            place = (head * group + j) * HEAD_WIDTH
-            att[:, place:place + HEAD_WIDTH] = normed[j * rows:(j + 1) * rows]
-
-    for start, size in tiles_of(features, 512):
-        picked = jnp.dot(
-            spread, att[:, start:start + size], preferred_element_type=jnp.float32
-        )
+            place = head * group + j
+            lse = jnp.where(head_lane == place, column[j * tall:(j + 1) * tall], lse)
+            for other in range(n_ctx):
+                first = j * tall + other * slots
+                part_out[other, :, place * HEAD_WIDTH:(place + 1) * HEAD_WIDTH] = mixed[
+                    first:first + live
+                ].astype(jnp.bfloat16)
+    for other in range(n_ctx):
+        lse_out[other] = lse[other * slots:(other + 1) * slots]
+
+    def give_back(other):
+        for copy in back_copies(ctx, other):
+            copy.start()
+
+    upper(give_back)
+    push_own(2, 4)
+
+    def take_back(other):
+        for copy in back_copies(other, other):
+            copy.wait_recv()
+
+    lower(take_back)
+    for other in range(n_ctx):
+        @pl.when(other < ctx)
+        def _():
+            part_all[other, :live] = part_got[other].astype(jnp.float32)
+            lse_all[other] = lse_in[other]
+
+        @pl.when(other == ctx)
+        def _():
+            part_all[other, :live] = part_out[other].astype(jnp.float32)
+            lse_all[other] = lse_out[other]
+
+    peak = jnp.max(lse_all[...], axis=0)
+    shares = [jnp.exp2(lse_all[other] - peak) for other in range(n_ctx)]
+    share_total = functools.reduce(jnp.add, shares)
+    shares = [share / share_total for share in shares]
+    for place in range(kv_heads * group):
+        span = slice(place * HEAD_WIDTH, (place + 1) * HEAD_WIDTH)
+        picked = shares[0][:, place:place + 1] * part_all[0, :, span]
+        for other in range(1, n_ctx):
+            picked = picked + shares[other][:, place:place + 1] * part_all[other, :, span]
         for expert in range(n_ep):
-            out_rows[expert, :, start:start + size] = picked[
-                expert * CAP:(expert + 1) * CAP
-            ].astype(jnp.bfloat16)
+            out_rows[expert, :, span] = picked[expert * CAP:(expert + 1) * CAP].astype(
+                jnp.bfloat16
+            )
 
     def row_copy(other, source):
         return pltpu.make_async_remote_copy(
@@ -236,6 +331,8 @@
 
     others(lambda other: row_copy(other, me).start())
     in_rows[me] = out_rows[ep]
+    process(ctx)
+    relay(ctx - 1, 0, 2)
     for copy in w_copies:
         copy.wait()
     others(lambda other: row_copy(other, other).wait_recv())
@@ -271,6 +368,7 @@
         )
         copy.start()
         part_copies.append(copy)
+    relay(ctx - 1, 2, 4)
     score_copy.wait()
     gain = jax.nn.sigmoid(
         score[:, :1].astype(jnp.float32) + score_in[:, :1].astype(jnp.float32)
@@ -306,27 +404,47 @@
     down_in[me] = down_out[me]
     returned[...] = jnp.zeros_like(returned)
 
+    def visit(step, carry):
+        block = ctx - step
+
+        @pl.when(step > 1)
+        def _():
+            relay(block, 0, 4)
+
+        @pl.when(block >= 0)
+        def _():
+            process(block)
+
+        return carry
+
+    lax.fori_loop(1, n_ctx, visit, 0)
+
+    for head in range(kv_heads):
+        normed = (acc[head] / totals[head]).astype(jnp.bfloat16)
+        for j in range(group):
+            place = (head * group + j) * HEAD_WIDTH
+            att[:, place:place + HEAD_WIDTH] = normed[j * rows:(j + 1) * rows]
+
     others(lambda other: row_copy(other, me).wait_send())
-    for copy in kv_copies(ctx, 0, 0, True) + kv_copies(ctx, 1, 1, True):
-        copy.wait_send()
-    if fan > 1:
-        for copy in kv_copies(ctx, 1, 0, True) + kv_copies(ctx, 0, 1, True):
+    lower(lambda other: q_copy(ctx, other).wait_send())
+
+    def sent_back(other):
+        for copy in back_copies(ctx, other):
             copy.wait_send()
 
+    upper(sent_back)
+
     def drain(step, carry):
-        from_left = (ctx + n_ctx - step) % n_ctx
-        from_right = (ctx + step) % n_ctx
-        for copy in kv_copies(from_left, 0, 0, False) + kv_copies(from_right, 1, 1, False):
-            copy.wait_send()
-
-        @pl.when(step + 1 < fan)
-        def _():
-            for copy in kv_copies(from_left, 1, 0, False) + kv_copies(from_right, 0, 1, False):
-                copy.wait_send()
+        block = ctx - step
+
+        @pl.when((ctx < n_ctx - 1) & (block >= 0))
+        def _():
+            for piece in range(4):
+                block_piece(block, piece).wait_send()
 
         return carry
 
-    lax.fori_loop(1, fan, drain, 0)
+    lax.fori_loop(0, n_ctx, drain, 0)
 
     others(lambda other: down_copy(other, other).wait_recv())
     for expert in range(n_ep):
@@ -356,7 +474,8 @@
     chunk_width = min(hidden_width, 256)
     chunk_count = hidden_width // chunk_width
     members = n * CAP
-    slots = -(-n_ep * CAP // 8) * 8
+    live = n_ep * CAP
+    slots = -(-live // 8) * 8
     bf16, f32 = jnp.bfloat16, jnp.float32
     vmem = pl.BlockSpec(memory_space=pltpu.VMEM)
     hbm = pl.BlockSpec(memory_space=pl.ANY)
@@ -376,6 +495,15 @@
             pltpu.VMEM((kv_heads, group * rows, HEAD_WIDTH), f32),
             pltpu.VMEM((kv_heads, group * rows, HEAD_WIDTH), f32),
             pltpu.VMEM((rows, features), bf16),
+            pltpu.VMEM((live, features), bf16),
+            pltpu.VMEM((n_ctx, live, features), bf16),
+            pltpu.VMEM((n_ctx * slots, features), f32),
+            pltpu.VMEM((n_ctx, live, features), bf16),
+            pltpu.VMEM((n_ctx, live, features), bf16),
+            pltpu.VMEM((n_ctx, slots, features), f32),
+            pltpu.VMEM((n_ctx, slots, 128), f32),
+            pltpu.VMEM((n_ctx, slots, 128), f32),
+            pltpu.VMEM((n_ctx, slots, 128), f32),
             pltpu.VMEM((n_ep, CAP, features), bf16),
             pltpu.VMEM((n, CAP, features), bf16),
             pltpu.VMEM((members, features), f32),
@@ -388,8 +516,8 @@
             pltpu.VMEM((n, CAP, features), bf16),
             pltpu.VMEM((slots, features), f32),
             dma((3,)),
-            dma((2, n_ctx, 2, 2)),
-            dma((n_ctx, 2, 2)),
+            dma((n_ctx, 4)),
+            dma((n_ctx, 4)),
             dma((n,)),
             dma((n,)),
             dma((chunk_count,)),
@@ -397,6 +525,12 @@
             dma((2,)),
             dma((n,)),
             dma((n,)),
+            dma((n_ctx,)),
+            dma((n_ctx,)),
+            dma((n_ctx,)),
+            dma((n_ctx,)),
+            dma((n_ctx,)),
+            dma((n_ctx,)),
         ],
         compiler_params=pltpu.CompilerParams(
             collective_id=0, has_side_effects=True, vmem_limit_bytes=60 * 1024 * 1024

time: 43.2 us -> 35.8 us (0.83)
  the two profiles are of different devices: /device:TPU:0 before, /device:TPU:27 now
where the time goes in v2:
time: 35.8 us; the launch traced here: 35.6 us
  Pallas kernels  33.6 us (94%)
  local copies, waits for them, and re-layouts  1.97 us (6%)
    pallas_call x1, Pallas kernels, shards(): pl.pallas_call(functools.partial(kernel, n_ctx, n_ep, n_tp), out_shape=ja...  33.6 us
    unnamed x1, local copies, waits for them, and re-layouts  1.97 us

profile of v2, /device:TPU:27, one launch (start us, length us, event | category | flops | bytes accessed | tf_op | source)
XLA Modules:
  0.0 35.6 jit_solution(14679559660340991104)
XLA Ops:
  0.0 33.6 %shard_map.82 = bf16[1,128,2560]{2,1,0:T(8,128)(2,1)} custom-call(s32[1,128]{1,0:T(1,128)} %bitcast.3, bf16[1,2560]{1,0:T(2,128)(2,1)} %bitcast.2, bf16[1,128,2560]{2,1,0:T(8,128)(2,1)} %q_ref.1, bf16[1,128,512]{2,1,0:T(8,128)(2,1)} %k_ref.1, bf16[1,128,512]{2,1,0:T(8,128)(2,1)} %v_ref.1, bf16[1,2560,1024]{2,1,0:T(8,128)(2,1)} %wg_hbm.1, ...), custom_call_target="tpu_custom_call" | custom-call | tf_op jit(solution)/shard_map/pallas_call | solution.py:483
  33.6 2.0 %copy.10 = bf16[1,128,2560]{2,1,0:T(8,128)(2,1)} copy(bf16[1,128,2560]{2,1,0:T(8,128)(2,1)} %shard_map.82) | data formatting | bytes 1310720

commit v3 on v2

--- a/solution.py
+++ b/solution.py
@@ -53,6 +53,7 @@
     chunk_count, _, double_width = part.shape
     chunk_width = double_width // 2
     slots = returned.shape[0]
+    places = features // HEAD_WIDTH
 
     w_copies = [
         pltpu.make_async_copy(src.at[0], dst, w_sem.at[index])
@@ -61,6 +62,22 @@
     for copy in w_copies:
         copy.start()
 
+    barrier = pltpu.get_barrier_semaphore()
+
+    def greet(other):
+        @pl.when(other != me)
+        def _():
+            pl.semaphore_signal(
+                barrier, inc=1,
+                device_id={"ep": other // n_ctx, "ctx": other % n_ctx},
+                device_id_type=MESH,
+            )
+
+    each(n, greet)
+    for step in range(1, n_tp):
+        pl.semaphore_signal(
+            barrier, inc=1, device_id={"tp": (tp + step) % n_tp}, device_id_type=MESH
+        )
     ids = ids_ref[...]
     slot_row = lax.broadcasted_iota(jnp.int32, (slots, rows), 0)
     choose = jnp.where(ids == slot_row, 1.0, 0.0)
@@ -85,22 +102,6 @@
         q_all[own_span, start:start + size] = picked
         q_out[:, start:start + size] = picked[:live].astype(jnp.bfloat16)
 
-    barrier = pltpu.get_barrier_semaphore()
-
-    def greet(other):
-        @pl.when(other != me)
-        def _():
-            pl.semaphore_signal(
-                barrier, inc=1,
-                device_id={"ep": other // n_ctx, "ctx": other % n_ctx},
-                device_id_type=MESH,
-            )
-
-    each(n, greet)
-    for step in range(1, n_tp):
-        pl.semaphore_signal(
-            barrier, inc=1, device_id={"tp": (tp + step) % n_tp}, device_id_type=MESH
-        )
     pl.semaphore_wait(barrier, n - 1 + n_tp - 1)
 
     def own_copy(piece):
@@ -307,7 +308,7 @@
         for other in range(1, n_ctx):
             picked = picked + shares[other][:, place:place + 1] * part_all[other, :, span]
         for expert in range(n_ep):
-            out_rows[expert, :, span] = picked[expert * CAP:(expert + 1) * CAP].astype(
+            out_rows[expert, place * CAP:(place + 1) * CAP] = picked[expert * CAP:(expert + 1) * CAP].astype(
                 jnp.bfloat16
             )
 
@@ -332,13 +333,18 @@
     others(lambda other: row_copy(other, me).start())
     in_rows[me] = out_rows[ep]
     process(ctx)
-    relay(ctx - 1, 0, 2)
+    relay(ctx - 1, 0, 4)
     for copy in w_copies:
         copy.wait()
     others(lambda other: row_copy(other, other).wait_recv())
 
     def gather_member(index):
-        members_f32[index * CAP:(index + 1) * CAP, :] = in_rows[index].astype(jnp.float32)
+        dense = in_rows[index].astype(jnp.float32)
+        for place in range(places):
+            span = slice(place * HEAD_WIDTH, (place + 1) * HEAD_WIDTH)
+            members_f32[index * CAP:(index + 1) * CAP, span] = dense[
+                place * CAP:(place + 1) * CAP
+            ]
 
     for index in range(n):
         gather_member(index)
@@ -368,7 +374,7 @@
         )
         copy.start()
         part_copies.append(copy)
-    relay(ctx - 1, 2, 4)
+    relay(ctx - 2, 0, 2)
     score_copy.wait()
     gain = jax.nn.sigmoid(
         score[:, :1].astype(jnp.float32) + score_in[:, :1].astype(jnp.float32)
@@ -386,9 +392,11 @@
             hidden[...], wd[:, start:start + size], preferred_element_type=jnp.float32
         )
         for index in range(n):
-            down_out[index, :, start:start + size] = product[
-                index * CAP:(index + 1) * CAP
-            ].astype(jnp.bfloat16)
+            for place in range(start // HEAD_WIDTH, (start + size) // HEAD_WIDTH):
+                lane = place * HEAD_WIDTH - start
+                down_out[index, place * CAP:(place + 1) * CAP] = product[
+                    index * CAP:(index + 1) * CAP, lane:lane + HEAD_WIDTH
+                ].astype(jnp.bfloat16)
 
     def down_copy(other, source):
         return pltpu.make_async_remote_copy(
@@ -407,7 +415,11 @@
     def visit(step, carry):
         block = ctx - step
 
-        @pl.when(step > 1)
+        @pl.when(step == 2)
+        def _():
+            relay(block, 2, 4)
+
+        @pl.when(step > 2)
         def _():
             relay(block, 0, 4)
 
@@ -451,7 +463,12 @@
         total = down_in[expert * n_ctx].astype(jnp.float32)
         for index in range(1, n_ctx):
             total = total + down_in[expert * n_ctx + index].astype(jnp.float32)
-        returned[expert * CAP:(expert + 1) * CAP, :] = total.astype(jnp.bfloat16).astype(jnp.float32)
+        total = total.astype(jnp.bfloat16).astype(jnp.float32)
+        for place in range(places):
+            span = slice(place * HEAD_WIDTH, (place + 1) * HEAD_WIDTH)
+            returned[expert * CAP:(expert + 1) * CAP, span] = total[
+                place * CAP:(place + 1) * CAP
+            ]
     for start, size in tiles_of(features, 512):
         routed = lax.dot_general(
             spread, returned[:, start:start + size].astype(jnp.bfloat16),
@@ -474,6 +491,7 @@
     chunk_width = min(hidden_width, 256)
     chunk_count = hidden_width // chunk_width
     members = n * CAP
+    dense = features // HEAD_WIDTH * CAP
     live = n_ep * CAP
     slots = -(-live // 8) * 8
     bf16, f32 = jnp.bfloat16, jnp.float32
@@ -504,16 +522,16 @@
             pltpu.VMEM((n_ctx, slots, 128), f32),
             pltpu.VMEM((n_ctx, slots, 128), f32),
             pltpu.VMEM((n_ctx, slots, 128), f32),
-            pltpu.VMEM((n_ep, CAP, features), bf16),
-            pltpu.VMEM((n, CAP, features), bf16),
+            pltpu.VMEM((n_ep, dense, HEAD_WIDTH), bf16),
+            pltpu.VMEM((n, dense, HEAD_WIDTH), bf16),
             pltpu.VMEM((members, features), f32),
             pltpu.VMEM((chunk_count, members, 2 * chunk_width), bf16),
             pltpu.VMEM((chunk_count, members, 2 * chunk_width), bf16),
             pltpu.VMEM((members, 128), bf16),
             pltpu.VMEM((members, 128), bf16),
             pltpu.VMEM((members, hidden_width), bf16),
-            pltpu.VMEM((n, CAP, features), bf16),
-            pltpu.VMEM((n, CAP, features), bf16),
+            pltpu.VMEM((n, dense, HEAD_WIDTH), bf16),
+            pltpu.VMEM((n, dense, HEAD_WIDTH), bf16),
             pltpu.VMEM((slots, features), f32),
             dma((3,)),
             dma((n_ctx, 4)),

time: 35.8 us -> 32.7 us (0.913)
  the two profiles are of different devices: /device:TPU:27 before, /device:TPU:0 now
where the time goes in v3:
time: 32.7 us; the launch traced here: 32.3 us
  Pallas kernels  30.3 us (93%)
  local copies, waits for them, and re-layouts  1.97 us (6%)
    pallas_call x1, Pallas kernels, shards(): pl.pallas_call(functools.partial(kernel, n_ctx, n_ep, n_tp), out_shape=ja...  30.3 us
    unnamed x1, local copies, waits for them, and re-layouts  1.97 us

profile of v3, /device:TPU:0, one launch (start us, length us, event | category | flops | bytes accessed | tf_op | source)
XLA Modules:
  0.0 32.3 jit_solution(15914343871489998575)
XLA Ops:
  0.0 30.3 %shard_map.82 = bf16[1,128,2560]{2,1,0:T(8,128)(2,1)} custom-call(s32[1,128]{1,0:T(1,128)} %bitcast.3, bf16[1,2560]{1,0:T(2,128)(2,1)} %bitcast.2, bf16[1,128,2560]{2,1,0:T(8,128)(2,1)} %q_ref.1, bf16[1,128,512]{2,1,0:T(8,128)(2,1)} %k_ref.1, bf16[1,128,512]{2,1,0:T(8,128)(2,1)} %v_ref.1, bf16[1,2560,1024]{2,1,0:T(8,128)(2,1)} %wg_hbm.1, ...), custom_call_target="tpu_custom_call" | custom-call | tf_op jit(solution)/shard_map/pallas_call | solution.py:501
  30.3 2.0 %copy.10 = bf16[1,128,2560]{2,1,0:T(8,128)(2,1)} copy(bf16[1,128,2560]{2,1,0:T(8,128)(2,1)} %shard_map.82) | data formatting | bytes 1310720
